TPU v7x, 32 devices: a whole 2x2x4 slice. The times are simulated.
32 devices in a mesh: dp: 8 (over z, core), ctx: 4 (over y, x).
Axes of the slice: x: 2, y: 2, z: 4, core: 2. Of those that a mesh axis runs over, the one named last changes fastest.
Arguments:
- qkv: bfloat16 [8, 512, 5120], P('dp', 'ctx'), may hold values from -8 to 8
- dest: int32 [8, 8], P('dp'), may hold values from 0 to 7, as said below
- order: int32 [8], replicated, may hold values from 0 to 7, as said below
- lengths: int32 [8, 8], replicated, may hold values from 1 to 256, 512 in all within a row
Outputs:
- attended: bfloat16 [8, 512, 4096], P('dp', 'ctx')
Inputs may be any that keep to these rules, and one draw needn't show every extreme that they name: `dest`: entry [r, s] is r itself, r + 1 or r - 1 (indices modulo 8), and the relation is mutual: if entry [r, s] is t, entry [t, s] is r. For every c below 4: order[2 c] is below 4 and order[2 c + 1] = 7 - order[2 c]; every span appears once.
All inputs are finite; a program needn't handle non-finite values.
Results may differ from a plain program's by a relative error of at most 0.0031.
Values may be sent and summed in bfloat16 or wider, within the bound.
A program may use at most 64 MiB of HBM per device.

v0:
```python
import functools
import math

import jax
import jax.numpy as jnp
from jax import lax
from jax.experimental import pallas as pl
from jax.experimental.pallas import tpu as pltpu
from jax.sharding import PartitionSpec as P

QUERY_HEADS = 32
KEY_VALUE_HEADS = 4
HEAD_SIZE = 128
QUERIES_PER_KV = 8
CHUNK_HEADS = 4
PLACE_PARTS = 4

MASK_FLOOR = -1e30
MESH = pl.DeviceIdType.MESH


def kernel(
    dp_count, ctx_count,
    qkv_ref, dest_hbm, order_hbm, lengths_hbm,
    out_ref,
    dest_ref, order_ref, lengths_ref, q_buf, kv_buf, bias, settled_bias, own, from_below, from_above,
    moved_q, moved_kv, own_kv,
    local_sem, scalar_sem, kv_send, kv_recv, out_send, out_recv, moved_send, moved_recv, corner_sem,
):
    dp_index = lax.axis_index("dp")
    me = lax.axis_index("ctx")
    above = lax.rem(dp_index + 1, dp_count)
    below = lax.rem(dp_index + dp_count - 1, dp_count)
    rows = qkv_ref.shape[1]
    span = rows // 2
    docs = lengths_ref.shape[1]
    query_width = QUERY_HEADS * HEAD_SIZE
    chunk_cols = CHUNK_HEADS * HEAD_SIZE
    moved = KEY_VALUE_HEADS - 1
    group_chunks = QUERIES_PER_KV // CHUNK_HEADS
    chunks = moved * group_chunks
    moved_cols = pl.ds(moved * QUERIES_PER_KV * HEAD_SIZE, QUERIES_PER_KV * HEAD_SIZE)
    my_rows = pl.ds(pl.multiple_of(me * rows, rows), rows)

    square = ctx_count == 4
    corner = 3

    def target_of(k):
        if square:
            return (me + 1 - 2 * lax.rem(me, 2), lax.rem(me + 2, 4), 3 - me)[k - 1]
        return lax.rem(me + k, ctx_count)

    def origin_of(k):
        return target_of(k) if square else lax.rem(me + ctx_count - k, ctx_count)

    barrier = pltpu.get_barrier_semaphore()
    pl.semaphore_signal(barrier, inc=1, device_id={"dp": above}, device_id_type=MESH)
    pl.semaphore_signal(barrier, inc=1, device_id={"dp": below}, device_id_type=MESH)
    for k in range(1, corner if square else ctx_count):
        pl.semaphore_signal(barrier, inc=1, device_id={"ctx": target_of(k)}, device_id_type=MESH)
    scalars = [
        pltpu.make_async_copy(source, target, scalar_sem.at[i])
        for i, (source, target) in enumerate(
            ((dest_hbm, dest_ref), (order_hbm, order_ref), (lengths_hbm, lengths_ref))
        )
    ]
    local = []
    for g in (moved, *range(moved)):
        for part in range(2):
            first = query_width + (part * KEY_VALUE_HEADS + g) * HEAD_SIZE
            copy = pltpu.make_async_copy(
                qkv_ref.at[0, :, pl.ds(first, HEAD_SIZE)],
                own_kv.at[part] if g == moved else kv_buf.at[g, part, my_rows, :],
                local_sem.at[2 * g + part],
            )
            copy.start()
            local.append(copy)
        if g == moved:
            q_copy = pltpu.make_async_copy(
                qkv_ref.at[0, :, pl.ds(0, query_width)], q_buf, local_sem.at[2 * KEY_VALUE_HEADS]
            )
            q_copy.start()
    for copy in scalars:
        copy.start()

    pl.semaphore_wait(barrier, 4 if square else ctx_count + 1)
    if square:
        pl.semaphore_signal(corner_sem, inc=1, device_id={"ctx": target_of(1)}, device_id_type=MESH)

    def kv_copy(g, k):
        peer = target_of(k)
        return pltpu.make_async_remote_copy(
            src_ref=kv_buf.at[g, :, my_rows, :],
            dst_ref=kv_buf.at[g, :, my_rows, :],
            send_sem=kv_send.at[g, k],
            recv_sem=kv_recv.at[g, k],
            device_id={"ctx": peer},
            device_id_type=MESH,
        )

    def kv_arrival(g, k):
        peer = origin_of(k)
        its_rows = pl.ds(pl.multiple_of(peer * rows, rows), rows)
        landed = kv_buf.at[g, :, its_rows, :]
        return pltpu.make_async_remote_copy(
            src_ref=landed, dst_ref=landed, send_sem=kv_send.at[g, k], recv_sem=kv_recv.at[g, k],
            device_id={"ctx": peer}, device_id_type=MESH,
        )

    def moved_copy(kind, up):
        return pltpu.make_async_remote_copy(
            src_ref=q_buf.at[:, moved_cols] if kind else own_kv,
            dst_ref=(moved_q if kind else moved_kv).at[up],
            send_sem=moved_send.at[up, kind],
            recv_sem=moved_recv.at[up, kind],
            device_id={"dp": above if up else below},
            device_id_type=MESH,
        )

    local[0].wait()
    local[1].wait()
    moved_copy(0, 1).start()
    moved_copy(0, 0).start()
    for g in range(moved):
        local[2 * g + 2].wait()
        local[2 * g + 3].wait()
        for k in range(1, ctx_count):
            if g == 0 and k == ctx_count - 1:
                q_copy.wait()
                moved_copy(1, 1).start()
                moved_copy(1, 0).start()
                if square:
                    pl.semaphore_wait(corner_sem, 1)
            kv_copy(g, k).start()

    for copy in scalars:
        copy.wait()

    def ends_of(sequence):
        ends = []
        total_length = 0
        for d in range(docs):
            total_length = total_length + lengths_ref[sequence, d]
            ends.append(total_length)
        return ends

    own_ends = ends_of(dp_index)

    def identity_of(place, first_slot, settled):
        early = place < span
        position = jnp.where(
            early, order_ref[first_slot] * span, order_ref[first_slot + 1] * span - span
        ) + place
        partners = dest_ref[0, first_slot], dest_ref[0, first_slot + 1]
        counted = jnp.where(early, partners[0] * docs, partners[1] * docs)
        if settled:
            ends = [jnp.where(early, *pair) for pair in zip(ends_of(partners[0]), ends_of(partners[1]))]
        else:
            ends = own_ends
        for end in ends:
            counted = counted + (position >= end).astype(jnp.int32)
        return position, counted

    query_place = lax.broadcasted_iota(jnp.int32, (rows, rows), 0)
    key_place = lax.broadcasted_iota(jnp.int32, (1, rows), 1)
    for settled, target in ((False, bias), (True, settled_bias)):
        query_position, query_document = identity_of(query_place, 2 * me, settled)
        for b in range(ctx_count):
            key_position, key_document = identity_of(key_place, 2 * b, settled)
            visible = (key_document == query_document) & (key_position <= query_position)
            target[:, b * rows:(b + 1) * rows] = jnp.where(visible, 0.0, MASK_FLOOR)

    row_source = jnp.where(
        lax.broadcasted_iota(jnp.int32, (rows, HEAD_SIZE), 0) < span,
        dest_ref[0, 2 * me], dest_ref[0, 2 * me + 1],
    )
    is_below = row_source == below
    is_above = row_source == above

    def settle_rows(kept, lower, upper):
        chosen = jnp.where(
            is_below, lower.astype(jnp.float32),
            jnp.where(is_above, upper.astype(jnp.float32), kept.astype(jnp.float32)),
        )
        return chosen.astype(jnp.bfloat16)

    def out_copy(chunk, up):
        return pltpu.make_async_remote_copy(
            src_ref=own.at[chunk],
            dst_ref=(from_below if up else from_above).at[chunk],
            send_sem=out_send.at[up, chunk],
            recv_sem=out_recv.at[up, chunk],
            device_id={"dp": above if up else below},
            device_id_type=MESH,
        )

    def send(chunk):
        out_copy(chunk, 1).start()
        out_copy(chunk, 0).start()

    exponent_scale = math.log2(math.e) / math.sqrt(HEAD_SIZE)

    def attend(query, g, mask):
        scores = lax.dot_general(
            query, kv_buf[g, 0], (((1,), (1,)), ((), ())), preferred_element_type=jnp.float32
        ) + mask[...]
        row_max = jnp.max(scores, axis=1, keepdims=True)
        weights = jnp.exp2((scores - row_max) * exponent_scale)
        total = jnp.sum(weights, axis=1, keepdims=True)
        mixed = jnp.dot(
            weights.astype(jnp.bfloat16), kv_buf[g, 1], preferred_element_type=jnp.float32
        )
        return (mixed / total).astype(jnp.bfloat16)

    for g in range(moved):
        for k in range(1, ctx_count):
            kv_arrival(g, k).wait_recv()

        def one_chunk(i, carry):
            chunk = g * group_chunks + i
            for j in range(CHUNK_HEADS):
                first = pl.multiple_of(chunk * chunk_cols + j * HEAD_SIZE, HEAD_SIZE)
                own[chunk, :, j * HEAD_SIZE:(j + 1) * HEAD_SIZE] = attend(
                    q_buf[:, pl.ds(first, HEAD_SIZE)], g, bias
                )
                if j == 0:
                    if g == 0:
                        @pl.when(i > 0)
                        def _():
                            send(chunk - 1)
                    else:
                        send(chunk - 1)
            return carry

        if g == moved - 1:
            for k in range(1, ctx_count):
                kv_copy(moved, k).start()
        lax.fori_loop(0, group_chunks, one_chunk, 0)
        if g == max(moved - 2, 0):
            moved_copy(0, 1).wait_recv()
            moved_copy(0, 0).wait_recv()
            for part in range(2):
                kv_buf[moved, part, my_rows, :] = settle_rows(
                    own_kv[part], moved_kv[1, part], moved_kv[0, part]
                )
    send(chunks - 1)

    moved_copy(1, 1).wait_recv()
    moved_copy(1, 0).wait_recv()
    for k in range(1, ctx_count):
        kv_arrival(moved, k).wait_recv()

    def one_moved(i, carry):
        for j in range(CHUNK_HEADS):
            inner = pl.ds(pl.multiple_of(i * chunk_cols + j * HEAD_SIZE, HEAD_SIZE), HEAD_SIZE)
            outer = pl.ds(
                pl.multiple_of(chunks * chunk_cols + i * chunk_cols + j * HEAD_SIZE, HEAD_SIZE),
                HEAD_SIZE,
            )
            query = settle_rows(q_buf[:, outer], moved_q[1, :, inner], moved_q[0, :, inner])
            out_ref[0, :, outer] = attend(query, moved, settled_bias)
        return carry

    lax.fori_loop(0, group_chunks, one_moved, 0)

    def settle(chunk, carry):
        out_copy(chunk, 1).wait_recv()
        out_copy(chunk, 0).wait_recv()
        for j in range(CHUNK_HEADS):
            first = pl.multiple_of(chunk * chunk_cols + j * HEAD_SIZE, HEAD_SIZE)
            part = pl.ds(j * HEAD_SIZE, HEAD_SIZE)
            out_ref[0, :, pl.ds(first, HEAD_SIZE)] = settle_rows(
                own[chunk, :, part], from_below[chunk, :, part], from_above[chunk, :, part]
            )
        return carry

    lax.fori_loop(0, chunks, settle, 0)

    for kind in range(2):
        for up in range(2):
            moved_copy(kind, up).wait_send()
    for g in range(KEY_VALUE_HEADS):
        for k in range(1, ctx_count):
            kv_copy(g, k).wait_send()

    def drain(chunk, carry):
        out_copy(chunk, 1).wait_send()
        out_copy(chunk, 0).wait_send()
        return carry

    lax.fori_loop(0, chunks, drain, 0)


def place_kernel(settled_ref, out_ref, sems):
    rows = settled_ref.shape[1] // PLACE_PARTS
    copies = [
        pltpu.make_async_copy(
            settled_ref.at[0, pl.ds(i * rows, rows), :],
            out_ref.at[0, pl.ds(i * rows, rows), :],
            sems.at[i],
        )
        for i in range(PLACE_PARTS)
    ]
    for copy in copies:
        copy.start()
    for copy in copies:
        copy.wait()


def on_device(dp_count, ctx_count, qkv, dest, order, lengths):
    rows = qkv.shape[1]
    query_width = QUERY_HEADS * HEAD_SIZE
    group_width = QUERIES_PER_KV * HEAD_SIZE
    chunks = (QUERY_HEADS - QUERIES_PER_KV) // CHUNK_HEADS
    chunk_shape = (chunks, rows, CHUNK_HEADS * HEAD_SIZE)
    keys = ctx_count * rows
    qkv, dest, order, lengths = (
        pltpu.with_memory_space_constraint(array, pltpu.HBM)
        for array in (qkv, dest, order, lengths)
    )
    settled = pl.pallas_call(
        functools.partial(kernel, dp_count, ctx_count),
        out_shape=pltpu.VMEM((1, rows, query_width), jnp.bfloat16),
        in_specs=[pl.BlockSpec(memory_space=pltpu.HBM)] * 4,
        out_specs=pl.BlockSpec(memory_space=pltpu.VMEM),
        scratch_shapes=[
            pltpu.SMEM(dest.shape, jnp.int32),
            pltpu.SMEM(order.shape, jnp.int32),
            pltpu.SMEM(lengths.shape, jnp.int32),
            pltpu.VMEM((rows, query_width), jnp.bfloat16),
            pltpu.VMEM((KEY_VALUE_HEADS, 2, keys, HEAD_SIZE), jnp.bfloat16),
            pltpu.VMEM((rows, keys), jnp.float32),
            pltpu.VMEM((rows, keys), jnp.float32),
            pltpu.VMEM(chunk_shape, jnp.bfloat16),
            pltpu.VMEM(chunk_shape, jnp.bfloat16),
            pltpu.VMEM(chunk_shape, jnp.bfloat16),
            pltpu.VMEM((2, rows, group_width), jnp.bfloat16),
            pltpu.VMEM((2, 2, rows, HEAD_SIZE), jnp.bfloat16),
            pltpu.VMEM((2, rows, HEAD_SIZE), jnp.bfloat16),
            pltpu.SemaphoreType.DMA((2 * KEY_VALUE_HEADS + 1,)),
            pltpu.SemaphoreType.DMA((3,)),
            pltpu.SemaphoreType.DMA((KEY_VALUE_HEADS, ctx_count)),
            pltpu.SemaphoreType.DMA((KEY_VALUE_HEADS, ctx_count)),
            pltpu.SemaphoreType.DMA((2, chunks)),
            pltpu.SemaphoreType.DMA((2, chunks)),
            pltpu.SemaphoreType.DMA((2, 2)),
            pltpu.SemaphoreType.DMA((2, 2)),
            pltpu.SemaphoreType.REGULAR,
        ],
        compiler_params=pltpu.CompilerParams(collective_id=0, has_side_effects=True,
            vmem_limit_bytes=40 << 20),
    )(qkv, dest, order, lengths)
    return pl.pallas_call(
        place_kernel,
        out_shape=jax.ShapeDtypeStruct((1, rows, query_width), jnp.bfloat16),
        in_specs=[pl.BlockSpec(memory_space=pltpu.VMEM)],
        out_specs=pl.BlockSpec(memory_space=pltpu.HBM),
        scratch_shapes=[pltpu.SemaphoreType.DMA((PLACE_PARTS,))],
        compiler_params=pltpu.CompilerParams(vmem_limit_bytes=8 << 20),
    )(settled)


def solution(mesh):
    return jax.shard_map(
        functools.partial(on_device, mesh.shape["dp"], mesh.shape["ctx"]),
        mesh=mesh,
        in_specs=(P("dp", "ctx", None), P("dp", None), P(), P()),
        out_specs=P("dp", "ctx", None),
        check_vma=False,
    )
```

profile of v0, /device:TPU:1, one launch (start us, length us, event | category | flops | bytes accessed | tf_op | source)
XLA Modules:
  0.0 32.0 jit_solution(724420133928795413)
XLA Ops:
  0.0 31.0 %shard_map.46.settled_ref = bf16[1,128,4096]{2,1,0:T(8,128)(2,1)S(1)} custom-call(bf16[1,128,5120]{2,1,0:T(8,128)(2,1)} %qkv_ref.1, s32[1,8]{1,0:T(1,128)} %dest_hbm.1, s32[8]{0:T(128)} %order_hbm.1, s32[8,8]{1,0:T(8,128)} %lengths_hbm.1), custom_call_target="tpu_custom_call" | custom-call | tf_op jit(solution)/shard_map/pallas_call | solution.py:321
  31.0 1.0 %shard_map.47 = bf16[1,128,4096]{2,1,0:T(8,128)(2,1)} custom-call(bf16[1,128,4096]{2,1,0:T(8,128)(2,1)S(1)} %shard_map.46.settled_ref), custom_call_target="tpu_custom_call" | custom-call | tf_op jit(solution)/shard_map/pallas_call | solution.py:353
where the time goes:
time: 32.2 us; the launch traced here: 32 us
  Pallas kernels  32 us (99%)
    pallas_call x1, Pallas kernels, on_device(): pl.pallas_call(functools.partial(kernel, dp_count, ctx_count), out_shape=...  31 us
    pallas_call x1, Pallas kernels, on_device(): pl.pallas_call(place_kernel, out_shape=jax.ShapeDtypeStruct((1, rows, que...  1 us

commit v1 on v0

v1 whole, which is shorter than its diff:
```python
import functools
import math

import jax
import jax.numpy as jnp
from jax import lax
from jax.experimental import pallas as pl
from jax.experimental.pallas import tpu as pltpu
from jax.sharding import PartitionSpec as P

QUERY_HEADS = 32
KEY_VALUE_HEADS = 4
HEAD_SIZE = 128
QUERIES_PER_KV = 8
UNIT_HEADS = 4
PLACE_PARTS = 4
LAST_BATCHES = (4, 2, 1, 1)

MASK_FLOOR = -1e30
MESH = pl.DeviceIdType.MESH


def batches_of(units):
    return (units - sum(LAST_BATCHES), *LAST_BATCHES)


def batch_of(unit, starts):
    return sum(unit >= start for start in starts[1:])


def kernel(
    dp_count, ctx_count,
    qkv_ref, dest_hbm, order_hbm, lengths_hbm,
    out_ref,
    dest_ref, order_ref, lengths_ref, q_buf, kv_buf,
    early_bias, late_bias, settled_early_bias, settled_late_bias,
    own, arrived, moved_q, moved_kv, own_kv,
    local_sem, kv_send, kv_recv, out_send, out_recv, moved_send, moved_recv, corner_sem,
):
    dp_index = lax.axis_index("dp")
    me = lax.axis_index("ctx")
    above = lax.rem(dp_index + 1, dp_count)
    below = lax.rem(dp_index + dp_count - 1, dp_count)
    span = qkv_ref.shape[1]
    keys = ctx_count * span
    docs = lengths_ref.shape[1]
    query_width = QUERY_HEADS * HEAD_SIZE
    unit_cols = UNIT_HEADS * HEAD_SIZE
    moved = KEY_VALUE_HEADS - 1
    group_units = QUERIES_PER_KV // UNIT_HEADS
    units = moved * 2 * group_units
    batches = batches_of(units)
    starts = [sum(batches[:n]) for n in range(len(batches))]
    moved_first = moved * QUERIES_PER_KV * HEAD_SIZE
    moved_cols = pl.ds(moved_first, QUERIES_PER_KV * HEAD_SIZE)
    my_rows = pl.ds(pl.multiple_of(me * span, span), span)

    square = ctx_count == 4

    def target_of(k):
        if square:
            return (me + 1 - 2 * lax.rem(me, 2), lax.rem(me + 2, 4), 3 - me)[k - 1]
        return lax.rem(me + k, ctx_count)

    def origin_of(k):
        return target_of(k) if square else lax.rem(me + ctx_count - k, ctx_count)

    barrier = pltpu.get_barrier_semaphore()
    pl.semaphore_signal(barrier, inc=1, device_id={"dp": above}, device_id_type=MESH)
    pl.semaphore_signal(barrier, inc=1, device_id={"dp": below}, device_id_type=MESH)
    for k in range(1, 3 if square else ctx_count):
        pl.semaphore_signal(barrier, inc=1, device_id={"ctx": target_of(k)}, device_id_type=MESH)
    scalars = [
        pltpu.make_async_copy(source, target, sem)
        for source, target, sem in (
            (dest_hbm, dest_ref, out_send.at[0]),
            (order_hbm, order_ref, out_send.at[1]),
            (lengths_hbm, lengths_ref, local_sem.at[3]),
        )
    ]
    def load(first, width, target, sem):
        pltpu.make_async_copy(qkv_ref.at[:, :, pl.ds(first, width)], target, local_sem.at[sem]).start()

    def loaded(target, sem):
        pltpu.make_async_copy(target, target, local_sem.at[sem]).wait()

    def load_kv(g, target, sem):
        for part in range(2):
            first = query_width + (part * KEY_VALUE_HEADS + g) * HEAD_SIZE
            load(first, HEAD_SIZE, target.at[part], sem)

    later_kv = kv_buf.at[pl.ds(1, moved - 1), :, :, my_rows, :]
    load_kv(moved, own_kv, 0)
    load_kv(0, kv_buf.at[0, :, :, my_rows, :], 1)
    load(moved_first, query_width - moved_first, q_buf.at[:, :, moved_cols], 2)
    for copy in scalars:
        copy.start()

    pl.semaphore_wait(barrier, 4 if square else ctx_count + 1)
    if square:
        pl.semaphore_signal(corner_sem, inc=1, device_id={"ctx": target_of(1)}, device_id_type=MESH)

    first_late = KEY_VALUE_HEADS

    def block_of(index, rows):
        if index == 0:
            return kv_buf.at[0, :, 0, rows, :]
        if index == first_late:
            return kv_buf.at[0, :, 1, rows, :]
        return kv_buf.at[index, :, :, rows, :]

    def kv_copy(index, k):
        block = block_of(index, my_rows)
        return pltpu.make_async_remote_copy(
            src_ref=block, dst_ref=block, send_sem=kv_send, recv_sem=kv_recv.at[index],
            device_id={"ctx": target_of(k)}, device_id_type=MESH,
        )

    def others_of(index):
        return block_of(index, pl.ds(0, (ctx_count - 1) * span))

    def wait_bytes(ref, sem):
        pltpu.make_async_copy(ref, ref, sem).wait()

    def moved_copy(kind, up):
        return pltpu.make_async_remote_copy(
            src_ref=q_buf.at[:, :, moved_cols] if kind else own_kv,
            dst_ref=(moved_q if kind else moved_kv).at[up],
            send_sem=moved_send.at[kind],
            recv_sem=moved_recv.at[kind],
            device_id={"dp": above if up else below},
            device_id_type=MESH,
        )

    loaded(own_kv, 0)
    moved_copy(0, 1).start()
    moved_copy(0, 0).start()
    loaded(kv_buf.at[0, :, :, my_rows, :], 1)
    for k in range(1, ctx_count):
        if k == ctx_count - 1:
            loaded(q_buf.at[:, :, moved_cols], 2)
            moved_copy(1, 1).start()
            moved_copy(1, 0).start()
            if square:
                pl.semaphore_wait(corner_sem, 1)
        kv_copy(0, k).start()
    for k in range(1, ctx_count):
        kv_copy(first_late, k).start()

    first_cols = pl.ds(0, moved_first)
    load(0, moved_first, q_buf.at[:, :, first_cols], 2)
    for g in range(1, moved):
        load_kv(g, kv_buf.at[g, :, :, my_rows, :], 1)
    for copy in scalars:
        copy.wait()

    def ends_of(sequence):
        ends = []
        total_length = 0
        for d in range(docs):
            total_length = total_length + lengths_ref[sequence, d]
            ends.append(total_length)
        return ends

    own_ends = ends_of(dp_index)

    def identity_of(place, slots, settled):
        first = place < span
        position = jnp.where(
            first, order_ref[slots[0]] * span, order_ref[slots[1]] * span - span
        ) + place
        partners = dest_ref[0, slots[0]], dest_ref[0, slots[1]]
        counted = jnp.where(first, partners[0] * docs, partners[1] * docs)
        if settled:
            ends = [jnp.where(first, *pair) for pair in zip(ends_of(partners[0]), ends_of(partners[1]))]
        else:
            ends = own_ends
        for end in ends:
            counted = counted + (position >= end).astype(jnp.int32)
        return position, counted

    query_place = lax.broadcasted_iota(jnp.int32, (2 * span, 2 * span), 0)
    key_place = lax.broadcasted_iota(jnp.int32, (1, 2 * span), 1)

    def build_bias(settled, early_target, late_target):
        query_position, query_document = identity_of(query_place, (2 * me, 2 * me + 1), settled)
        for half in range(2):
            for b in range(0, ctx_count, 2):
                key_position, key_document = identity_of(
                    key_place, (2 * b + half, 2 * b + 2 + half), settled
                )
                visible = (key_document == query_document) & (key_position <= query_position)
                mask = jnp.where(visible, 0.0, MASK_FLOOR)
                if half == 0:
                    early_target[:, b * span:(b + 2) * span] = mask[:span]
                late_target[:, half * keys + b * span:half * keys + (b + 2) * span] = mask[span:]

    build_bias(False, early_bias, late_bias)
    loaded(later_kv, 1)
    for g in range(1, moved):
        for k in range(1, ctx_count):
            kv_copy(g, k).start()
    build_bias(True, settled_early_bias, settled_late_bias)
    loaded(q_buf.at[:, :, first_cols], 2)

    def settle_rows(half, kept, lower, upper):
        source = dest_ref[0, 2 * me + half]
        chosen = jnp.where(
            source == below, lower.astype(jnp.float32),
            jnp.where(source == above, upper.astype(jnp.float32), kept.astype(jnp.float32)),
        )
        return chosen.astype(jnp.bfloat16)

    def send(unit, batch):
        for up in range(2):
            pltpu.make_async_remote_copy(
                src_ref=own.at[unit],
                dst_ref=arrived.at[unit, up],
                send_sem=out_send.at[up],
                recv_sem=out_recv.at[batch],
                device_id={"dp": above if up else below},
                device_id_type=MESH,
            ).start()

    def send_one(unit):
        if isinstance(unit, int):
            send(unit, batch_of(unit, starts))
            return
        batch = sum((unit >= start).astype(jnp.int32) for start in starts[1:])
        send(unit, batch)

    exponent_scale = math.log2(math.e) / math.sqrt(HEAD_SIZE)

    def attend(queries, g, half, mask, between=None):
        width = keys * (1 + half)
        stacked = jnp.concatenate(queries, axis=0)
        key_rows, value_rows = (
            kv_buf[g, part].reshape(width, HEAD_SIZE) if half else kv_buf[g, part, 0]
            for part in range(2)
        )
        scores = lax.dot_general(
            stacked, key_rows, (((1,), (1,)), ((), ())), preferred_element_type=jnp.float32
        )
        if between is not None:
            between()
        scores = scores.reshape(len(queries), span, width) + mask[...][None]
        scores = scores.reshape(len(queries) * span, width)
        row_max = jnp.max(scores, axis=1, keepdims=True)
        weights = jnp.exp2((scores - row_max) * exponent_scale)
        total = jnp.sum(weights, axis=1, keepdims=True)
        mixed = jnp.dot(
            weights.astype(jnp.bfloat16), value_rows, preferred_element_type=jnp.float32
        )
        mixed = (mixed / total).astype(jnp.bfloat16)
        return [mixed[j * span:(j + 1) * span] for j in range(len(queries))]

    def head_cols(first, j):
        return pl.ds(pl.multiple_of(first + j * HEAD_SIZE, HEAD_SIZE), HEAD_SIZE)

    for g in range(moved):
        for half in range(2):
            if g == 0 or half == 0:
                index = first_late if g == 0 and half else g
                wait_bytes(others_of(index), kv_recv.at[index])

            def one_unit(i, carry):
                unit = (2 * g + half) * group_units + i
                first = (g * group_units + i) * unit_cols

                def send_last():
                    if g == 0 and half == 0:
                        @pl.when(i > 0)
                        def _():
                            send_one(unit - 1)
                    else:
                        send_one(unit - 1)

                heads = attend(
                    [q_buf[half, :, head_cols(first, j)] for j in range(UNIT_HEADS)],
                    g, half, late_bias if half else early_bias, send_last,
                )
                for j, head in enumerate(heads):
                    own[unit, :, j * HEAD_SIZE:(j + 1) * HEAD_SIZE] = head
                return carry

            if g == moved - 1 and half == 0:
                for k in range(1, ctx_count):
                    kv_copy(moved, k).start()
            lax.fori_loop(0, group_units, one_unit, 0)
        if g == max(moved - 2, 0):
            wait_bytes(moved_kv, moved_recv.at[0])
            for part in range(2):
                for half in range(2):
                    kv_buf[moved, part, half, my_rows, :] = settle_rows(
                        half, own_kv[part, half], moved_kv[1, part, half], moved_kv[0, part, half]
                    )
    send_one(units - 1)

    wait_bytes(moved_q, moved_recv.at[1])
    wait_bytes(others_of(moved), kv_recv.at[moved])

    for half in range(2):
        def one_moved(i, carry):
            queries = []
            for j in range(UNIT_HEADS):
                inner = head_cols(i * unit_cols, j)
                queries.append(settle_rows(
                    half, q_buf[half, :, head_cols(moved_first + i * unit_cols, j)],
                    moved_q[1, half, :, inner], moved_q[0, half, :, inner],
                ))
            heads = attend(queries, moved, half, settled_late_bias if half else settled_early_bias)
            for j, head in enumerate(heads):
                out_ref[half, :, head_cols(moved_first + i * unit_cols, j)] = head
            return carry

        lax.fori_loop(0, group_units, one_moved, 0)

    wait_bytes(moved_kv, moved_send.at[0])
    wait_bytes(moved_q, moved_send.at[1])
    wait_bytes(kv_buf.at[:, :, :, pl.ds(0, (ctx_count - 1) * span), :], kv_send)

    def settle(unit, carry):
        half = lax.rem(lax.div(unit, group_units), 2)
        first = (lax.div(unit, 2 * group_units) * group_units + lax.rem(unit, group_units)) * unit_cols
        for j in range(UNIT_HEADS):
            part = pl.ds(j * HEAD_SIZE, HEAD_SIZE)
            out_ref[half, :, head_cols(first, j)] = settle_rows(
                half, own[unit, :, part], arrived[unit, 1, :, part], arrived[unit, 0, :, part]
            )
        return carry

    for batch, (start, size) in enumerate(zip(starts, batches)):
        if batch == len(batches) - 1:
            for up in range(2):
                wait_bytes(own, out_send.at[up])
        wait_bytes(arrived.at[pl.ds(start, size)], out_recv.at[batch])
        lax.fori_loop(start, start + size, settle, 0)


def place_kernel(settled_ref, out_ref, sems):
    rows = settled_ref.shape[1] // (PLACE_PARTS // 2)
    copies = [
        pltpu.make_async_copy(
            settled_ref.at[half, pl.ds(i * rows, rows), :],
            out_ref.at[half, pl.ds(i * rows, rows), :],
            sems.at[half * (PLACE_PARTS // 2) + i],
        )
        for half in range(2) for i in range(PLACE_PARTS // 2)
    ]
    for copy in copies:
        copy.start()
    for copy in copies:
        copy.wait()


def on_device(dp_count, ctx_count, qkv, dest, order, lengths):
    span = qkv.shape[1] // 2
    query_width = QUERY_HEADS * HEAD_SIZE
    group_width = QUERIES_PER_KV * HEAD_SIZE
    units = 2 * (QUERY_HEADS - QUERIES_PER_KV) // UNIT_HEADS
    unit_shape = (units, span, UNIT_HEADS * HEAD_SIZE)
    keys = ctx_count * span
    qkv = qkv.reshape(2, span, qkv.shape[2])
    qkv, dest, order, lengths = (
        pltpu.with_memory_space_constraint(array, pltpu.HBM)
        for array in (qkv, dest, order, lengths)
    )
    settled = pl.pallas_call(
        functools.partial(kernel, dp_count, ctx_count),
        out_shape=pltpu.VMEM((2, span, query_width), jnp.bfloat16),
        in_specs=[pl.BlockSpec(memory_space=pltpu.HBM)] * 4,
        out_specs=pl.BlockSpec(memory_space=pltpu.VMEM),
        scratch_shapes=[
            pltpu.SMEM(dest.shape, jnp.int32),
            pltpu.SMEM(order.shape, jnp.int32),
            pltpu.SMEM(lengths.shape, jnp.int32),
            pltpu.VMEM((2, span, query_width), jnp.bfloat16),
            pltpu.VMEM((KEY_VALUE_HEADS, 2, 2, keys, HEAD_SIZE), jnp.bfloat16),
            pltpu.VMEM((span, keys), jnp.float32),
            pltpu.VMEM((span, 2 * keys), jnp.float32),
            pltpu.VMEM((span, keys), jnp.float32),
            pltpu.VMEM((span, 2 * keys), jnp.float32),
            pltpu.VMEM(unit_shape, jnp.bfloat16),
            pltpu.VMEM((units, 2, *unit_shape[1:]), jnp.bfloat16),
            pltpu.VMEM((2, 2, span, group_width), jnp.bfloat16),
            pltpu.VMEM((2, 2, 2, span, HEAD_SIZE), jnp.bfloat16),
            pltpu.VMEM((2, 2, span, HEAD_SIZE), jnp.bfloat16),
            pltpu.SemaphoreType.DMA((4,)),
            pltpu.SemaphoreType.DMA,
            pltpu.SemaphoreType.DMA((KEY_VALUE_HEADS + 1,)),
            pltpu.SemaphoreType.DMA((2,)),
            pltpu.SemaphoreType.DMA((len(batches_of(units)),)),
            pltpu.SemaphoreType.DMA((2,)),
            pltpu.SemaphoreType.DMA((2,)),
            pltpu.SemaphoreType.REGULAR,
        ],
        compiler_params=pltpu.CompilerParams(collective_id=0, has_side_effects=True,
            vmem_limit_bytes=40 << 20),
    )(qkv, dest, order, lengths)
    placed = pl.pallas_call(
        place_kernel,
        out_shape=jax.ShapeDtypeStruct((2, span, query_width), jnp.bfloat16),
        in_specs=[pl.BlockSpec(memory_space=pltpu.VMEM)],
        out_specs=pl.BlockSpec(memory_space=pltpu.HBM),
        scratch_shapes=[pltpu.SemaphoreType.DMA((PLACE_PARTS,))],
        compiler_params=pltpu.CompilerParams(vmem_limit_bytes=8 << 20),
    )(settled)
    return placed.reshape(1, 2 * span, query_width)


def solution(mesh):
    return jax.shard_map(
        functools.partial(on_device, mesh.shape["dp"], mesh.shape["ctx"]),
        mesh=mesh,
        in_specs=(P("dp", "ctx", None), P("dp", None), P(), P()),
        out_specs=P("dp", "ctx", None),
        check_vma=False,
    )
```

time: 32.2 us -> 31.1 us (0.966); the launches traced: 32 us -> 30.6 us
  Pallas kernels: 32 us -> 30.6 us
    pallas_call x1, Pallas kernels: 31 us -> 29.6 us  [on_device(): pl.pallas_call(functools.partial(kernel, dp_count, ctx_count), out_shape=...]
where the time goes in v1:
time: 31.1 us; the launch traced here: 30.6 us
  Pallas kernels  30.6 us (98%)
    pallas_call x1, Pallas kernels, on_device(): pl.pallas_call(functools.partial(kernel, dp_count, ctx_count), out_shape=...  29.6 us
    pallas_call x1, Pallas kernels, on_device(): pl.pallas_call(place_kernel, out_shape=jax.ShapeDtypeStruct((2, span, que...  1 us

profile of v1, /device:TPU:1, one launch (start us, length us, event | category | flops | bytes accessed | tf_op | source)
XLA Modules:
  0.0 30.6 jit_solution(241392491572934801)
XLA Ops:
  0.0 29.6 %shard_map.46.settled_ref = bf16[2,64,4096]{2,1,0:T(8,128)(2,1)S(1)} custom-call(bf16[2,64,5120]{2,1,0:T(8,128)(2,1)} %bitcast.2, s32[1,8]{1,0:T(1,128)} %dest_hbm.1, s32[8]{0:T(128)} %order_hbm.1, s32[8,8]{1,0:T(8,128)} %lengths_hbm.1), custom_call_target="tpu_custom_call" | custom-call | tf_op jit(solution)/shard_map/pallas_call | solution.py:368
  29.6 1.0 %shard_map.47 = bf16[2,64,4096]{2,1,0:T(8,128)(2,1)} custom-call(bf16[2,64,4096]{2,1,0:T(8,128)(2,1)S(1)} %shard_map.46.settled_ref), custom_call_target="tpu_custom_call" | custom-call | tf_op jit(solution)/shard_map/pallas_call | solution.py:400

commit v2 on v1

--- a/solution.py
+++ b/solution.py
@@ -14,7 +14,7 @@
 QUERIES_PER_KV = 8
 UNIT_HEADS = 4
 PLACE_PARTS = 4
-LAST_BATCHES = (4, 2, 1, 1)
+LAST_BATCHES = (2, 2)
 
 MASK_FLOOR = -1e30
 MESH = pl.DeviceIdType.MESH
@@ -211,23 +211,26 @@
         )
         return chosen.astype(jnp.bfloat16)
 
-    def send(unit, batch):
+    odd = lax.rem(dp_index, 2)
+    closing = (dp_index == 0) | (dp_index == dp_count - 1)
+
+    def send(start, count, part="all"):
+        some = pl.ds(start, count)
         for up in range(2):
-            pltpu.make_async_remote_copy(
-                src_ref=own.at[unit],
-                dst_ref=arrived.at[unit, up],
+            copy = pltpu.make_async_remote_copy(
+                src_ref=own.at[some],
+                dst_ref=arrived.at[up, some],
                 send_sem=out_send.at[up],
-                recv_sem=out_recv.at[batch],
+                recv_sem=out_recv.at[batch_of(start, starts)],
                 device_id={"dp": above if up else below},
                 device_id_type=MESH,
-            ).start()
-
-    def send_one(unit):
-        if isinstance(unit, int):
-            send(unit, batch_of(unit, starts))
-            return
-        batch = sum((unit >= start).astype(jnp.int32) for start in starts[1:])
-        send(unit, batch)
+            )
+            if part == "all":
+                copy.start()
+            elif part == "prompt":
+                pl.when((odd != up) | closing)(copy.start)
+            else:
+                pl.when((odd == up) & jnp.logical_not(closing))(copy.start)
 
     exponent_scale = math.log2(math.e) / math.sqrt(HEAD_SIZE)
 
@@ -263,21 +266,25 @@
                 index = first_late if g == 0 and half else g
                 wait_bytes(others_of(index), kv_recv.at[index])
 
+            phase = 2 * g + half
+            before = phase * group_units
+
             def one_unit(i, carry):
-                unit = (2 * g + half) * group_units + i
+                unit = before + i
                 first = (g * group_units + i) * unit_cols
 
-                def send_last():
-                    if g == 0 and half == 0:
-                        @pl.when(i > 0)
-                        def _():
-                            send_one(unit - 1)
-                    else:
-                        send_one(unit - 1)
+                def send_done():
+                    if g > 0:
+                        if phase > 2:
+                            pl.when(i == 0)(lambda: send(before - group_units, group_units))
+                        return
+                    for n in range(group_units):
+                        if before + n > 0:
+                            pl.when(i == n)(lambda: send(before + n - 1, 1, "prompt"))
 
                 heads = attend(
                     [q_buf[half, :, head_cols(first, j)] for j in range(UNIT_HEADS)],
-                    g, half, late_bias if half else early_bias, send_last,
+                    g, half, late_bias if half else early_bias, send_done,
                 )
                 for j, head in enumerate(heads):
                     own[unit, :, j * HEAD_SIZE:(j + 1) * HEAD_SIZE] = head
@@ -287,6 +294,9 @@
                 for k in range(1, ctx_count):
                     kv_copy(moved, k).start()
             lax.fori_loop(0, group_units, one_unit, 0)
+            if phase == 1:
+                send(before + group_units - 1, 1, "prompt")
+                send(0, before + group_units, "held")
         if g == max(moved - 2, 0):
             wait_bytes(moved_kv, moved_recv.at[0])
             for part in range(2):
@@ -294,7 +304,7 @@
                     kv_buf[moved, part, half, my_rows, :] = settle_rows(
                         half, own_kv[part, half], moved_kv[1, part, half], moved_kv[0, part, half]
                     )
-    send_one(units - 1)
+    send(units - group_units, group_units)
 
     wait_bytes(moved_q, moved_recv.at[1])
     wait_bytes(others_of(moved), kv_recv.at[moved])
@@ -325,7 +335,7 @@
         for j in range(UNIT_HEADS):
             part = pl.ds(j * HEAD_SIZE, HEAD_SIZE)
             out_ref[half, :, head_cols(first, j)] = settle_rows(
-                half, own[unit, :, part], arrived[unit, 1, :, part], arrived[unit, 0, :, part]
+                half, own[unit, :, part], arrived[1, unit, :, part], arrived[0, unit, :, part]
             )
         return carry
 
@@ -333,24 +343,23 @@
         if batch == len(batches) - 1:
             for up in range(2):
                 wait_bytes(own, out_send.at[up])
-        wait_bytes(arrived.at[pl.ds(start, size)], out_recv.at[batch])
+        wait_bytes(arrived.at[:, pl.ds(start, size)], out_recv.at[batch])
         lax.fori_loop(start, start + size, settle, 0)
 
 
-def place_kernel(settled_ref, out_ref, sems):
+def place_kernel(settled_ref, out_ref, sem):
     rows = settled_ref.shape[1] // (PLACE_PARTS // 2)
     copies = [
         pltpu.make_async_copy(
             settled_ref.at[half, pl.ds(i * rows, rows), :],
             out_ref.at[half, pl.ds(i * rows, rows), :],
-            sems.at[half * (PLACE_PARTS // 2) + i],
+            sem,
         )
         for half in range(2) for i in range(PLACE_PARTS // 2)
     ]
     for copy in copies:
         copy.start()
-    for copy in copies:
-        copy.wait()
+    pltpu.make_async_copy(settled_ref, out_ref, sem).wait()
 
 
 def on_device(dp_count, ctx_count, qkv, dest, order, lengths):
@@ -381,7 +390,7 @@
             pltpu.VMEM((span, keys), jnp.float32),
             pltpu.VMEM((span, 2 * keys), jnp.float32),
             pltpu.VMEM(unit_shape, jnp.bfloat16),
-            pltpu.VMEM((units, 2, *unit_shape[1:]), jnp.bfloat16),
+            pltpu.VMEM((2, *unit_shape), jnp.bfloat16),
             pltpu.VMEM((2, 2, span, group_width), jnp.bfloat16),
             pltpu.VMEM((2, 2, 2, span, HEAD_SIZE), jnp.bfloat16),
             pltpu.VMEM((2, 2, span, HEAD_SIZE), jnp.bfloat16),
@@ -402,7 +411,7 @@
         out_shape=jax.ShapeDtypeStruct((2, span, query_width), jnp.bfloat16),
         in_specs=[pl.BlockSpec(memory_space=pltpu.VMEM)],
         out_specs=pl.BlockSpec(memory_space=pltpu.HBM),
-        scratch_shapes=[pltpu.SemaphoreType.DMA((PLACE_PARTS,))],
+        scratch_shapes=[pltpu.SemaphoreType.DMA],
         compiler_params=pltpu.CompilerParams(vmem_limit_bytes=8 << 20),
     )(settled)
     return placed.reshape(1, 2 * span, query_width)

time: 31.1 us -> 30.8 us (level); the launches traced: 30.6 us -> 30.7 us
  no operation moved by 1% of the time
where the time goes in v2:
time: 30.8 us; the launch traced here: 30.7 us
  Pallas kernels  30.7 us (100%)
    pallas_call x1, Pallas kernels, on_device(): pl.pallas_call(functools.partial(kernel, dp_count, ctx_count), out_shape=...  29.7 us
    pallas_call x1, Pallas kernels, on_device(): pl.pallas_call(place_kernel, out_shape=jax.ShapeDtypeStruct((2, span, que...  0.97 us

profile of v2, /device:TPU:1, one launch (start us, length us, event | category | flops | bytes accessed | tf_op | source)
XLA Modules:
  0.0 30.7 jit_solution(15522205340284394444)
XLA Ops:
  0.0 29.7 %shard_map.46.settled_ref = bf16[2,64,4096]{2,1,0:T(8,128)(2,1)S(1)} custom-call(bf16[2,64,5120]{2,1,0:T(8,128)(2,1)} %bitcast.2, s32[1,8]{1,0:T(1,128)} %dest_hbm.1, s32[8]{0:T(128)} %order_hbm.1, s32[8,8]{1,0:T(8,128)} %lengths_hbm.1), custom_call_target="tpu_custom_call" | custom-call | tf_op jit(solution)/shard_map/pallas_call | solution.py:377
  29.7 1.0 %shard_map.47 = bf16[2,64,4096]{2,1,0:T(8,128)(2,1)} custom-call(bf16[2,64,4096]{2,1,0:T(8,128)(2,1)S(1)} %shard_map.46.settled_ref), custom_call_target="tpu_custom_call" | custom-call | tf_op jit(solution)/shard_map/pallas_call | solution.py:409

commit v3 on v2

--- a/solution.py
+++ b/solution.py
@@ -14,7 +14,7 @@
 QUERIES_PER_KV = 8
 UNIT_HEADS = 4
 PLACE_PARTS = 4
-LAST_BATCHES = (2, 2)
+LAST_BATCHES = (2,)
 
 MASK_FLOOR = -1e30
 MESH = pl.DeviceIdType.MESH
@@ -213,6 +213,8 @@
 
     odd = lax.rem(dp_index, 2)
     closing = (dp_index == 0) | (dp_index == dp_count - 1)
+    links_before = lax.div(jnp.where(odd == 1, dp_index, dp_count - 2 - dp_index), 2)
+    holds = jnp.logical_not(closing) & (links_before < dp_count // 2 - 2)
 
     def send(start, count, part="all"):
         some = pl.ds(start, count)
@@ -227,10 +229,9 @@
             )
             if part == "all":
                 copy.start()
-            elif part == "prompt":
-                pl.when((odd != up) | closing)(copy.start)
             else:
-                pl.when((odd == up) & jnp.logical_not(closing))(copy.start)
+                held = (odd == up) & holds
+                pl.when(held if part == "held" else jnp.logical_not(held))(copy.start)
 
     exponent_scale = math.log2(math.e) / math.sqrt(HEAD_SIZE)
 

time: 30.8 us -> 30.7 us (level)
  no operation moved by 1% of the time
where the time goes in v3:
time: 30.7 us; the launch traced here: 30.5 us
  Pallas kernels  30.5 us (99%)
    pallas_call x1, Pallas kernels, on_device(): pl.pallas_call(functools.partial(kernel, dp_count, ctx_count), out_shape=...  29.6 us
    pallas_call x1, Pallas kernels, on_device(): pl.pallas_call(place_kernel, out_shape=jax.ShapeDtypeStruct((2, span, que...  0.97 us

profile of v3, /device:TPU:1, one launch (start us, length us, event | category | flops | bytes accessed | tf_op | source)
XLA Modules:
  0.0 30.5 jit_solution(14438374305447694939)
XLA Ops:
  0.0 29.6 %shard_map.46.settled_ref = bf16[2,64,4096]{2,1,0:T(8,128)(2,1)S(1)} custom-call(bf16[2,64,5120]{2,1,0:T(8,128)(2,1)} %bitcast.2, s32[1,8]{1,0:T(1,128)} %dest_hbm.1, s32[8]{0:T(128)} %order_hbm.1, s32[8,8]{1,0:T(8,128)} %lengths_hbm.1), custom_call_target="tpu_custom_call" | custom-call | tf_op jit(solution)/shard_map/pallas_call | solution.py:378
  29.6 1.0 %shard_map.47 = bf16[2,64,4096]{2,1,0:T(8,128)(2,1)} custom-call(bf16[2,64,4096]{2,1,0:T(8,128)(2,1)S(1)} %shard_map.46.settled_ref), custom_call_target="tpu_custom_call" | custom-call | tf_op jit(solution)/shard_map/pallas_call | solution.py:410

commit v4 on v3

--- a/solution.py
+++ b/solution.py
@@ -75,14 +75,14 @@
         for source, target, sem in (
             (dest_hbm, dest_ref, out_send.at[0]),
             (order_hbm, order_ref, out_send.at[1]),
-            (lengths_hbm, lengths_ref, local_sem.at[3]),
+            (lengths_hbm, lengths_ref, local_sem.at[2]),
         )
     ]
     def load(first, width, target, sem):
-        pltpu.make_async_copy(qkv_ref.at[:, :, pl.ds(first, width)], target, local_sem.at[sem]).start()
+        pltpu.make_async_copy(qkv_ref.at[:, :, pl.ds(first, width)], target, sem).start()
 
     def loaded(target, sem):
-        pltpu.make_async_copy(target, target, local_sem.at[sem]).wait()
+        pltpu.make_async_copy(target, target, sem).wait()
 
     def load_kv(g, target, sem):
         for part in range(2):
@@ -90,9 +90,9 @@
             load(first, HEAD_SIZE, target.at[part], sem)
 
     later_kv = kv_buf.at[pl.ds(1, moved - 1), :, :, my_rows, :]
-    load_kv(moved, own_kv, 0)
-    load_kv(0, kv_buf.at[0, :, :, my_rows, :], 1)
-    load(moved_first, query_width - moved_first, q_buf.at[:, :, moved_cols], 2)
+    load_kv(moved, own_kv, kv_send)
+    load_kv(0, kv_buf.at[0, :, :, my_rows, :], local_sem.at[0])
+    load(moved_first, query_width - moved_first, q_buf.at[:, :, moved_cols], local_sem.at[1])
     for copy in scalars:
         copy.start()
 
@@ -126,19 +126,19 @@
         return pltpu.make_async_remote_copy(
             src_ref=q_buf.at[:, :, moved_cols] if kind else own_kv,
             dst_ref=(moved_q if kind else moved_kv).at[up],
-            send_sem=moved_send.at[kind],
+            send_sem=moved_send,
             recv_sem=moved_recv.at[kind],
             device_id={"dp": above if up else below},
             device_id_type=MESH,
         )
 
-    loaded(own_kv, 0)
+    loaded(own_kv, kv_send)
     moved_copy(0, 1).start()
     moved_copy(0, 0).start()
-    loaded(kv_buf.at[0, :, :, my_rows, :], 1)
+    loaded(kv_buf.at[0, :, :, my_rows, :], local_sem.at[0])
     for k in range(1, ctx_count):
         if k == ctx_count - 1:
-            loaded(q_buf.at[:, :, moved_cols], 2)
+            loaded(q_buf.at[:, :, moved_cols], local_sem.at[1])
             moved_copy(1, 1).start()
             moved_copy(1, 0).start()
             if square:
@@ -148,9 +148,9 @@
         kv_copy(first_late, k).start()
 
     first_cols = pl.ds(0, moved_first)
-    load(0, moved_first, q_buf.at[:, :, first_cols], 2)
+    load(0, moved_first, q_buf.at[:, :, first_cols], local_sem.at[1])
     for g in range(1, moved):
-        load_kv(g, kv_buf.at[g, :, :, my_rows, :], 1)
+        load_kv(g, kv_buf.at[g, :, :, my_rows, :], local_sem.at[0])
     for copy in scalars:
         copy.wait()
 
@@ -196,12 +196,12 @@
                 late_target[:, half * keys + b * span:half * keys + (b + 2) * span] = mask[span:]
 
     build_bias(False, early_bias, late_bias)
-    loaded(later_kv, 1)
+    loaded(later_kv, local_sem.at[0])
     for g in range(1, moved):
         for k in range(1, ctx_count):
             kv_copy(g, k).start()
     build_bias(True, settled_early_bias, settled_late_bias)
-    loaded(q_buf.at[:, :, first_cols], 2)
+    loaded(q_buf.at[:, :, first_cols], local_sem.at[1])
 
     def settle_rows(half, kept, lower, upper):
         source = dest_ref[0, 2 * me + half]
@@ -326,8 +326,8 @@
 
         lax.fori_loop(0, group_units, one_moved, 0)
 
-    wait_bytes(moved_kv, moved_send.at[0])
-    wait_bytes(moved_q, moved_send.at[1])
+    moved_units = (4 * QUERIES_PER_KV + 8) * HEAD_SIZE // unit_cols
+    wait_bytes(own.at[pl.ds(0, moved_units)], moved_send)
     wait_bytes(kv_buf.at[:, :, :, pl.ds(0, (ctx_count - 1) * span), :], kv_send)
 
     def settle(unit, carry):
@@ -395,12 +395,12 @@
             pltpu.VMEM((2, 2, span, group_width), jnp.bfloat16),
             pltpu.VMEM((2, 2, 2, span, HEAD_SIZE), jnp.bfloat16),
             pltpu.VMEM((2, 2, span, HEAD_SIZE), jnp.bfloat16),
-            pltpu.SemaphoreType.DMA((4,)),
+            pltpu.SemaphoreType.DMA((3,)),
             pltpu.SemaphoreType.DMA,
             pltpu.SemaphoreType.DMA((KEY_VALUE_HEADS + 1,)),
             pltpu.SemaphoreType.DMA((2,)),
             pltpu.SemaphoreType.DMA((len(batches_of(units)),)),
-            pltpu.SemaphoreType.DMA((2,)),
+            pltpu.SemaphoreType.DMA,
             pltpu.SemaphoreType.DMA((2,)),
             pltpu.SemaphoreType.REGULAR,
         ],

time: 30.7 us -> 30.7 us (level)
  no operation moved by 1% of the time
where the time goes in v4:
time: 30.7 us; the launch traced here: 30.5 us
  Pallas kernels  30.5 us (99%)
    pallas_call x1, Pallas kernels, on_device(): pl.pallas_call(functools.partial(kernel, dp_count, ctx_count), out_shape=...  29.5 us
    pallas_call x1, Pallas kernels, on_device(): pl.pallas_call(place_kernel, out_shape=jax.ShapeDtypeStruct((2, span, que...  0.97 us

profile of v4, /device:TPU:1, one launch (start us, length us, event | category | flops | bytes accessed | tf_op | source)
XLA Modules:
  0.0 30.5 jit_solution(12013008415384661393)
XLA Ops:
  0.0 29.5 %shard_map.46.settled_ref = bf16[2,64,4096]{2,1,0:T(8,128)(2,1)S(1)} custom-call(bf16[2,64,5120]{2,1,0:T(8,128)(2,1)} %bitcast.2, s32[1,8]{1,0:T(1,128)} %dest_hbm.1, s32[8]{0:T(128)} %order_hbm.1, s32[8,8]{1,0:T(8,128)} %lengths_hbm.1), custom_call_target="tpu_custom_call" | custom-call | tf_op jit(solution)/shard_map/pallas_call | solution.py:378
  29.5 1.0 %shard_map.47 = bf16[2,64,4096]{2,1,0:T(8,128)(2,1)} custom-call(bf16[2,64,4096]{2,1,0:T(8,128)(2,1)S(1)} %shard_map.46.settled_ref), custom_call_target="tpu_custom_call" | custom-call | tf_op jit(solution)/shard_map/pallas_call | solution.py:410

commit v5 on v4

--- a/solution.py
+++ b/solution.py
@@ -153,6 +153,10 @@
         load_kv(g, kv_buf.at[g, :, :, my_rows, :], local_sem.at[0])
     for copy in scalars:
         copy.wait()
+    loaded(later_kv, local_sem.at[0])
+    for g in range(1, moved):
+        for k in range(1, ctx_count):
+            kv_copy(g, k).start()
 
     def ends_of(sequence):
         ends = []
@@ -196,10 +200,6 @@
                 late_target[:, half * keys + b * span:half * keys + (b + 2) * span] = mask[span:]
 
     build_bias(False, early_bias, late_bias)
-    loaded(later_kv, local_sem.at[0])
-    for g in range(1, moved):
-        for k in range(1, ctx_count):
-            kv_copy(g, k).start()
     build_bias(True, settled_early_bias, settled_late_bias)
     loaded(q_buf.at[:, :, first_cols], local_sem.at[1])
 

time: 30.7 us -> 30.7 us (level)
  no operation moved by 1% of the time
where the time goes in v5:
time: 30.7 us; the launch traced here: 30.5 us
  Pallas kernels  30.5 us (99%)
    pallas_call x1, Pallas kernels, on_device(): pl.pallas_call(functools.partial(kernel, dp_count, ctx_count), out_shape=...  29.5 us
    pallas_call x1, Pallas kernels, on_device(): pl.pallas_call(place_kernel, out_shape=jax.ShapeDtypeStruct((2, span, que...  0.97 us

profile of v5, /device:TPU:1, one launch (start us, length us, event | category | flops | bytes accessed | tf_op | source)
XLA Modules:
  0.0 30.5 jit_solution(13647927199843450354)
XLA Ops:
  0.0 29.5 %shard_map.46.settled_ref = bf16[2,64,4096]{2,1,0:T(8,128)(2,1)S(1)} custom-call(bf16[2,64,5120]{2,1,0:T(8,128)(2,1)} %bitcast.2, s32[1,8]{1,0:T(1,128)} %dest_hbm.1, s32[8]{0:T(128)} %order_hbm.1, s32[8,8]{1,0:T(8,128)} %lengths_hbm.1), custom_call_target="tpu_custom_call" | custom-call | tf_op jit(solution)/shard_map/pallas_call | solution.py:378
  29.5 1.0 %shard_map.47 = bf16[2,64,4096]{2,1,0:T(8,128)(2,1)} custom-call(bf16[2,64,4096]{2,1,0:T(8,128)(2,1)S(1)} %shard_map.46.settled_ref), custom_call_target="tpu_custom_call" | custom-call | tf_op jit(solution)/shard_map/pallas_call | solution.py:410
